TPU v7x, 32 devices: a whole 2x2x4 slice. The times are simulated.
32 devices in a mesh: agent: 4 (over x, core), tile: 8 (over z, y).
Axes of the slice: x: 2, y: 2, z: 4, core: 2. Of those that a mesh axis runs over, the one named last changes fastest.
Arguments:
- states: float32 [4, 4, 512, 512], P('agent', None, 'tile'), may hold values from -6 to 6
- sinogram: float32 [256, 4, 128], P('tile'), may hold values from -6 to 6
- blocks: bfloat16 [2048, 128, 128], P('tile'), may hold values from -0.1875 to 0.1875
- block_angle: int32 [2048], P('tile'), may hold values from 0 to 63
- block_detector: int32 [2048], P('tile'), may hold values from 0 to 3
- block_tile: int32 [2048], P('tile'), may hold values from 0 to 255
- conv_first: bfloat16 [3, 3, 3, 32], replicated, may hold values from -3 to 3
- conv_hidden: bfloat16 [3, 2, 3, 3, 32, 32], replicated, may hold values from -0.5 to 0.5
- conv_last: bfloat16 [3, 3, 3, 32], replicated, may hold values from -0.375 to 0.375
Outputs:
- new_states: float32 [4, 4, 512, 512], P('agent', None, 'tile')
Inputs may be any that keep to these rules, and one draw needn't show every extreme that they name: `block_angle`: each block's angle index. `block_detector`: each block's detector block. `block_tile`: tile index among the 256 pixel tiles of the block's device.
All inputs are finite; a program needn't handle non-finite values.
Results may differ from a plain program's by a relative error of at most 0.0051.
Values may be sent and summed in bfloat16 or wider, within the bound.
A program may use at most 256 MiB of HBM per device.

v0:
```python
import functools

import jax
import jax.numpy as jnp
import numpy as np
from jax import lax
from jax.experimental import pallas as pl
from jax.experimental.pallas import tpu as pltpu
from jax.sharding import PartitionSpec as P

DATA_STEPS = 2
MESH = pl.DeviceIdType.MESH
LANES = 128
GROUPS = 16
STRIPS = 16


def extended(cells, axis, dim, width):
    count = lax.axis_size(axis)
    ends = count - 1
    head = lax.slice_in_dim(cells, 0, width, axis=dim)
    tail = lax.slice_in_dim(cells, cells.shape[dim] - width, cells.shape[dim], axis=dim)
    return jnp.concatenate(
        [
            lax.ppermute(tail, axis, [(i, (i + 1) % count) for i in range(ends)]),
            cells,
            lax.ppermute(head, axis, [((i + 1) % count, i) for i in range(ends)]),
        ],
        axis=dim,
    )


def band(weight, rows_in, first_row):
    taps_row = np.zeros((3, rows_in, 4), np.float32)
    for row_in in range(rows_in):
        for row in range(4):
            tap = row_in + first_row - row + 1
            if 0 <= tap < 3:
                taps_row[tap, row_in, row] = 1
    return spread(weight, taps_row)


def band_same(weight):
    parts = []
    for tap in range(3):
        taps_row = np.zeros((3, 4, 4), np.float32)
        taps_row[tap] = np.eye(4)
        parts.append(spread(weight, taps_row))
    return jnp.stack(parts)


def spread(weight, taps_row):
    taps_position = np.zeros((3, 4, 2), np.float32)
    for k in range(4):
        for par in range(2):
            if 0 <= k - par < 3:
                taps_position[k - par, k, par] = 1
    half = jnp.einsum("irs,ijcd->jrscd", jnp.asarray(taps_row, jnp.bfloat16), weight, preferred_element_type=jnp.float32)
    full = jnp.einsum(
        "jkp,jrscd->krcpsd", jnp.asarray(taps_position, jnp.bfloat16), half.astype(jnp.bfloat16), preferred_element_type=jnp.float32
    )
    return full.astype(jnp.bfloat16)


def hidden_band(weight):
    layers, _, _, inner, _ = weight.shape
    padded = jnp.pad(jnp.swapaxes(weight, 1, 2), ((0, 0), (1, 1), (2, 2), (0, 0), (0, 0)))
    parts = [padded[:, 1 - par : 5 - par, 3 - row : 7 - row] for par in range(2) for row in range(4)]
    return jnp.concatenate(parts, axis=-1).reshape(layers, 16 * inner, 8 * inner)


def hidden_same(weight):
    layers, _, _, inner, _ = weight.shape
    padded = jnp.pad(weight, ((0, 0), (0, 0), (1, 1), (0, 0), (0, 0)))
    wide = jnp.concatenate([padded[:, :, 1 - par : 5 - par] for par in range(2) for _ in range(4)], axis=-1)
    lane_row = (np.arange(8 * inner) // inner) % 4
    mask = jnp.asarray(lane_row[None, :] == np.arange(4)[:, None])
    full = jnp.where(mask[:, None, :], wide[:, :, :, None], jnp.zeros((), wide.dtype))
    return full.reshape(layers, 48 * inner, 8 * inner)


def net_weights(first, hidden, last, axial):
    inner = hidden.shape[-1]
    depth = 16 * inner
    if axial:
        w_first = band_same(first[:, :, None, :]).reshape(48, 8 * inner)
    else:
        w_first = band(first[:, :, None, :], 4, 0).reshape(16, 8 * inner)

    def last_part(weight):
        if axial:
            return band_same(weight).reshape(3 * depth, 8)
        return band(weight, 4, 0).reshape(depth, 8)

    w_hidden = hidden_same(hidden) if axial else hidden_band(hidden)
    w_last = jnp.tile(last_part(last[:, :, :, None]), (1, GROUPS))
    return w_first, w_hidden, w_last


def net_kernel(plan, x_ref, w1_ref, wh_ref, wl_ref, out_ref, even, odd):
    group, size, layers, masked, first_out, out_chunks = plan
    chunks = x_ref.shape[0]
    pairs = chunks * group
    step_rows = group * size

    if masked:
        place = lax.axis_index("tile")
        at_start = place == 0
        at_end = place == lax.axis_size("tile") - 1

    for side in range(2):
        for ref in (even, odd):
            ref[side, 0] = jnp.zeros(ref.shape[2:], ref.dtype)
            ref[side, pairs + 1] = jnp.zeros(ref.shape[2:], ref.dtype)

    def store(side, c, y):
        y = jnp.maximum(y, 0.0)
        if masked:
            outside = (at_start & (c < first_out)) | (at_end & (c >= chunks - first_out))
            y = y * jnp.where(outside, 0.0, 1.0)
        y = y.astype(jnp.bfloat16)
        even[side, pl.ds(1 + c * group, group)] = y[:, :LANES].reshape(group, size, LANES)
        odd[side, pl.ds(1 + c * group, group)] = y[:, LANES:].reshape(group, size, LANES)

    def gathered(side, c):
        low = c * group
        sources = ((odd, low), (even, low + 1), (odd, low + 1), (even, low + 2))
        parts = [ref[side, pl.ds(at, group)].reshape(step_rows, LANES) for ref, at in sources]
        return jnp.concatenate(parts, axis=1)

    def first_step(c, carry):
        y = lax.dot_general(
            x_ref[c], w1_ref[...], (((0,), (0,)), ((), ())), preferred_element_type=jnp.float32
        )
        store(0, c, y)
        return carry

    lax.fori_loop(0, chunks, first_step, 0)
    for layer in range(layers):
        source, target = layer % 2, (layer + 1) % 2

        def hidden_step(c, carry):
            y = jnp.dot(gathered(source, c), wh_ref[layer], preferred_element_type=jnp.float32)
            store(target, c, y)
            return carry

        lax.fori_loop(0, chunks, hidden_step, 0)

    lane_group = lax.broadcasted_iota(jnp.int32, (step_rows, LANES), 1) // 8

    def last_step(c, carry):
        y = jnp.dot(gathered(layers % 2, c + first_out), wl_ref[...], preferred_element_type=jnp.float32)
        out_ref[c // GROUPS] = jnp.where(lane_group == c % GROUPS, y, out_ref[c // GROUPS])
        return carry

    out_ref[...] = jnp.zeros_like(out_ref)
    lax.fori_loop(0, out_chunks, last_step, 0)


def run_net(x, weights, group, size, masked, first_out, out_chunks):
    w_first, w_hidden, w_last = weights
    chunks = x.shape[0]
    pairs = chunks * group
    layers = w_hidden.shape[0]
    out_blocks = -(-out_chunks // GROUPS)
    plan = (group, size, layers, masked, first_out, out_chunks)
    whole = pl.BlockSpec(memory_space=pltpu.VMEM)
    cells = pairs * size * 2 * LANES
    return pl.pallas_call(
        functools.partial(net_kernel, plan),
        out_shape=jax.ShapeDtypeStruct((out_blocks, group * size, LANES), jnp.float32),
        in_specs=[whole] * 4,
        out_specs=whole,
        scratch_shapes=[
            pltpu.VMEM((2, pairs + 2, size, LANES), jnp.bfloat16),
            pltpu.VMEM((2, pairs + 2, size, LANES), jnp.bfloat16),
        ],
        cost_estimate=pl.CostEstimate(flops=cells * 512 * 2 * 3, bytes_accessed=x.size * 2, transcendentals=0),
        compiler_params=pltpu.CompilerParams(vmem_limit_bytes=60 * 1024 * 1024),
        name="net_masked" if masked else "net_plain",
    )(x, w_first, w_hidden, w_last)


def axial_kernel(plan, x_ref, w1_ref, wh_ref, wl_ref, out_ref, even, odd):
    group, layers, halo = plan
    rows, _, cells = x_ref.shape
    pairs = cells // STRIPS
    step_rows = group * cells
    place = lax.axis_index("tile")
    at_start = place == 0
    at_end = place == lax.axis_size("tile") - 1
    strip = lax.broadcasted_iota(jnp.int32, (STRIPS, LANES), 0)

    for side in range(2):
        for ref in (even, odd):
            ref[side, 0] = jnp.zeros(ref.shape[2:], ref.dtype)
            ref[side, rows + 1] = jnp.zeros(ref.shape[2:], ref.dtype)

    def store(side, row, count, y):
        outside = (at_start & (row < halo)) | (at_end & (row >= rows - halo))
        y = jnp.maximum(y, 0.0) * jnp.where(outside, 0.0, 1.0)
        y = y.reshape(count, pairs, STRIPS, 2 * LANES)
        at = pl.ds(row + 1, count)
        even[side, at, pl.ds(1, pairs)] = y[..., :LANES].astype(jnp.bfloat16)
        odd[side, at, pl.ds(1, pairs)] = y[..., LANES:].astype(jnp.bfloat16)
        for r in range(count):
            before = y[r, pairs - 1, :, LANES:]
            before = jnp.where(strip == 0, 0.0, pltpu.roll(before, 1, 0))
            odd[side, row + 1 + r, 0] = before.astype(jnp.bfloat16)
            after = y[r, 0, :, :LANES]
            after = jnp.where(strip == STRIPS - 1, 0.0, pltpu.roll(after, STRIPS - 1, 0))
            even[side, row + 1 + r, pairs + 1] = after.astype(jnp.bfloat16)

    def gathered(side, row):
        parts = []
        for tap in range(3):
            at = pl.ds(row + tap, group)
            for ref, first in ((odd, 0), (even, 1), (odd, 1), (even, 2)):
                parts.append(ref[side, at, pl.ds(first, pairs)].reshape(step_rows, LANES))
        return jnp.concatenate(parts, axis=1)

    def first_step(row, carry):
        y = lax.dot_general(
            x_ref[row], w1_ref[...], (((0,), (0,)), ((), ())), preferred_element_type=jnp.float32
        )
        store(0, row, 1, y)
        return carry

    lax.fori_loop(0, rows, first_step, 0)
    for layer in range(layers):
        source, target = layer % 2, (layer + 1) % 2

        def hidden_step(c, carry):
            y = jnp.dot(gathered(source, c * group), wh_ref[layer], preferred_element_type=jnp.float32)
            store(target, c * group, group, y)
            return carry

        lax.fori_loop(0, rows // group, hidden_step, 0)

    lane_group = lax.broadcasted_iota(jnp.int32, (step_rows, LANES), 1) // 8

    def last_step(c, carry):
        y = jnp.dot(gathered(layers % 2, halo + c * group), wl_ref[...], preferred_element_type=jnp.float32)
        out_ref[c // GROUPS] = jnp.where(lane_group == c % GROUPS, y, out_ref[c // GROUPS])
        return carry

    out_ref[...] = jnp.zeros_like(out_ref)
    lax.fori_loop(0, (rows - 2 * halo) // group, last_step, 0)


def axial_net(rimmed, weights, halo):
    slices, rows, columns = rimmed.shape
    group = 4
    local = rows - 2 * halo
    pairs = columns // (2 * STRIPS)
    cells = pairs * STRIPS
    column = jnp.arange(columns, dtype=jnp.int32)[:, None, None, None]
    k = jnp.arange(4, dtype=jnp.int32)[None, :, None, None]
    i = jnp.arange(pairs, dtype=jnp.int32)[None, None, :, None]
    j = jnp.arange(STRIPS, dtype=jnp.int32)[None, None, None, :]
    place = (column == j * (2 * pairs) + 2 * i + k - 1).astype(jnp.bfloat16).reshape(columns, 4, cells)
    padded = jnp.pad(rimmed, ((0, 0), (1, 1), (0, 0)))
    x = jnp.einsum("zrc,ckm->kzrm", padded, place, preferred_element_type=jnp.float32).astype(jnp.bfloat16)
    x = jnp.stack([x[:, :, tap : tap + rows] for tap in range(3)])
    x = jnp.transpose(x, (3, 0, 1, 2, 4)).reshape(rows, 12 * slices, cells)
    layers = weights[1].shape[0]
    whole = pl.BlockSpec(memory_space=pltpu.VMEM)
    out_chunks = local // group
    out = pl.pallas_call(
        functools.partial(axial_kernel, (group, layers, halo)),
        out_shape=jax.ShapeDtypeStruct((-(-out_chunks // GROUPS), group * cells, LANES), jnp.float32),
        in_specs=[whole] * 4,
        out_specs=whole,
        scratch_shapes=[
            pltpu.VMEM((2, rows + 2, pairs + 2, STRIPS, LANES), jnp.bfloat16),
            pltpu.VMEM((2, rows + 2, pairs + 2, STRIPS, LANES), jnp.bfloat16),
        ],
        compiler_params=pltpu.CompilerParams(vmem_limit_bytes=60 * 1024 * 1024),
        name="net_axial",
    )(x, *weights)
    out = out.astype(jnp.bfloat16).reshape(out.shape[0], group, cells, LANES)
    out = jnp.swapaxes(out, 2, 3).reshape(out.shape[0], group, GROUPS, 2, slices, cells)
    net = jnp.einsum("bgqpzm,cpm->zbqgc", out, place[:, 1:3], preferred_element_type=jnp.float32)
    return net.reshape(slices, -1, columns)[:, :local]


def sagittal_net(rimmed, weights, halo):
    slices, rows, columns = rimmed.shape
    padded = jnp.pad(rimmed, ((0, 0), (1, 1), (0, 0)))
    x = jnp.stack([padded[:, k : k + rows : 2] for k in range(4)], axis=0)
    x = jnp.transpose(x, (2, 0, 1, 3)).reshape(rows // 2, 4 * slices, columns)
    local = rows - 2 * halo
    out = run_net(x, weights, 1, columns, True, halo // 2, local // 2)
    out = out.reshape(out.shape[0], columns, GROUPS, 2, slices)
    return jnp.transpose(out, (4, 0, 2, 3, 1)).reshape(slices, -1, columns)[:, :local]


def coronal_net(rounded, weights):
    slices, rows, columns = rounded.shape
    group = 512 // rows
    chunks = columns // (2 * group)
    turned = jnp.transpose(jnp.pad(rounded, ((0, 0), (0, 0), (1, 1))), (2, 0, 1))
    x = jnp.stack([turned[k : k + columns : 2] for k in range(4)], axis=1)
    x = x.reshape(chunks, group, 4 * slices, rows)
    x = jnp.transpose(x, (0, 2, 1, 3)).reshape(chunks, 4 * slices, group * rows)
    out = run_net(x, weights, group, rows, False, 0, chunks)
    out = out.reshape(out.shape[0], group, rows, GROUPS, 2, slices)
    return jnp.transpose(out, (5, 2, 0, 3, 1, 4)).reshape(slices, rows, -1)[:, :, :columns]


def ray_kernel(count, part_ref, sino_ref, out_ref, got, fresh, send1, recv1, send2, recv2):
    rows = sino_ref.shape[0]
    agent = lax.axis_index("agent")

    @pl.when(agent == 0)
    def _():
        me = lax.axis_index("tile")
        barrier = pltpu.get_barrier_semaphore()
        for d in range(1, count):
            pl.semaphore_signal(barrier, inc=1, device_id=(agent, lax.rem(me + d, count)), device_id_type=MESH)
        pl.semaphore_wait(barrier, count - 1)

        def part_copy(d):
            peer = lax.rem(me + d, count)
            return pltpu.make_async_remote_copy(
                src_ref=part_ref.at[peer],
                dst_ref=got.at[d],
                send_sem=send1.at[d],
                recv_sem=recv1.at[d],
                device_id=(agent, peer),
                device_id_type=MESH,
            )

        for d in range(1, count):
            part_copy(d).start()
        total = part_ref[me].astype(jnp.float32) - sino_ref[...]
        for d in range(1, count):
            part_copy(d).wait_recv()
            total = total + got[d].astype(jnp.float32)
        fresh[...] = total.astype(jnp.bfloat16)

        def rest_copy(d):
            return pltpu.make_async_remote_copy(
                src_ref=fresh,
                dst_ref=got2_slot(me),
                send_sem=send2.at[d],
                recv_sem=recv2.at[d],
                device_id=(agent, lax.rem(me + d, count)),
                device_id_type=MESH,
            )

        def got2_slot(slot):
            return out_ref.at[slot]

        for d in range(1, count):
            rest_copy(d).start()
        out_ref[me] = fresh[...]
        for d in range(1, count):
            rest_copy(d).wait_recv()
        for d in range(1, count):
            part_copy(d).wait_send()
            rest_copy(d).wait_send()

    @pl.when(agent != 0)
    def _():
        out_ref[...] = jnp.zeros_like(out_ref)


def ray_exchange(part, sinogram, count):
    rows = sinogram.shape[0]
    whole = pl.BlockSpec(memory_space=pltpu.VMEM)
    return pl.pallas_call(
        functools.partial(ray_kernel, count),
        out_shape=jax.ShapeDtypeStruct((count, rows, LANES), jnp.bfloat16),
        in_specs=[whole] * 2,
        out_specs=whole,
        scratch_shapes=[
            pltpu.VMEM((count, rows, LANES), jnp.bfloat16),
            pltpu.VMEM((rows, LANES), jnp.bfloat16),
            pltpu.SemaphoreType.DMA((count,)),
            pltpu.SemaphoreType.DMA((count,)),
            pltpu.SemaphoreType.DMA((count,)),
            pltpu.SemaphoreType.DMA((count,)),
        ],
        compiler_params=pltpu.CompilerParams(collective_id=0, has_side_effects=True),
        name="ray_exchange",
    )(part, sinogram)


def agent_kernel(own_ref, out_ref, near, pair, far, send, recv):
    me = lax.axis_index("agent")
    tile = lax.axis_index("tile")
    partner = me + 1 - 2 * (me % 2)
    across = (me + 2) % 4
    barrier = pltpu.get_barrier_semaphore()
    for peer in (partner, across):
        pl.semaphore_signal(barrier, inc=1, device_id=(peer, tile), device_id_type=MESH)
    pl.semaphore_wait(barrier, 2)

    first = pltpu.make_async_remote_copy(
        src_ref=own_ref,
        dst_ref=near,
        send_sem=send.at[0],
        recv_sem=recv.at[0],
        device_id=(partner, tile),
        device_id_type=MESH,
    )
    first.start()
    first.wait()
    pair[...] = (own_ref[...].astype(jnp.float32) + near[...].astype(jnp.float32)).astype(jnp.bfloat16)
    second = pltpu.make_async_remote_copy(
        src_ref=pair,
        dst_ref=far,
        send_sem=send.at[1],
        recv_sem=recv.at[1],
        device_id=(across, tile),
        device_id_type=MESH,
    )
    second.start()
    second.wait()
    out_ref[...] = near[...].astype(jnp.float32) + far[...].astype(jnp.float32)


def agent_sum(own):
    whole = pl.BlockSpec(memory_space=pltpu.VMEM)
    return pl.pallas_call(
        agent_kernel,
        out_shape=jax.ShapeDtypeStruct(own.shape, jnp.float32),
        in_specs=[whole],
        out_specs=whole,
        scratch_shapes=[
            pltpu.VMEM(own.shape, jnp.bfloat16),
            pltpu.VMEM(own.shape, jnp.bfloat16),
            pltpu.VMEM(own.shape, jnp.bfloat16),
            pltpu.SemaphoreType.DMA((2,)),
            pltpu.SemaphoreType.DMA((2,)),
        ],
        compiler_params=pltpu.CompilerParams(collective_id=1, has_side_effects=True),
        name="agent_sum",
    )(own)


def per_device(
    states,
    sinogram,
    blocks,
    block_angle,
    block_detector,
    block_tile,
    conv_first,
    conv_hidden,
    conv_last,
):
    current = states[0]
    slices, local_rows, image_columns = current.shape
    tile_count = lax.axis_size("tile")
    agent_place = lax.axis_index("agent")
    is_data = agent_place == 0
    tiles_here = local_rows * image_columns // LANES
    rays_here = sinogram.shape[0]
    ray_total = rays_here * tile_count
    part_shape = (tile_count, rays_here * slices, LANES)

    def ray_hot():
        ray_index = block_angle * (image_columns // LANES) + block_detector
        return ray_index[:, None] == jnp.arange(ray_total, dtype=jnp.int32)[None, :]

    def tile_hot():
        return block_tile[:, None] == jnp.arange(tiles_here, dtype=jnp.int32)[None, :]

    def project(volume):
        pixels = volume.astype(jnp.bfloat16).reshape(slices, tiles_here, LANES)
        picked = jnp.einsum(
            "bt,ztp->bzp", tile_hot().astype(jnp.bfloat16), pixels, preferred_element_type=jnp.float32
        ).astype(jnp.bfloat16)
        projected = jnp.einsum("bzp,bqp->bzq", picked, blocks, preferred_element_type=jnp.float32)
        partial_value = jnp.einsum(
            "br,bzq->rzq",
            ray_hot().astype(jnp.float32),
            projected,
            precision=lax.Precision.HIGHEST,
        )
        return partial_value.astype(jnp.bfloat16).reshape(part_shape)

    def spread_back(residual):
        residual = residual.reshape(ray_total, slices, LANES)
        picked = jnp.einsum(
            "br,rzq->bzq", ray_hot().astype(jnp.bfloat16), residual, preferred_element_type=jnp.float32
        ).astype(jnp.bfloat16)
        contribution = jnp.einsum("bzq,bqp->bzp", picked, blocks, preferred_element_type=jnp.float32)
        summed = jnp.einsum(
            "bt,bzp->ztp",
            tile_hot().astype(jnp.float32),
            contribution,
            precision=lax.Precision.HIGHEST,
        )
        return summed.reshape(slices, local_rows, image_columns)

    halo = conv_hidden.shape[1] + 2
    rounded = current.astype(jnp.bfloat16)
    rimmed = extended(rounded, "tile", 1, halo)
    no_part = jnp.zeros(part_shape, jnp.bfloat16)

    def reflect_of(net):
        return 2.0 * (current - net) - current

    def weights_of(o):
        return net_weights(conv_first[o], conv_hidden[o], conv_last[o], o == 0)

    def data_start():
        return project(current), current

    def axial_only():
        return no_part, reflect_of(axial_net(rimmed, weights_of(0), halo))

    def sagittal_only():
        return no_part, reflect_of(sagittal_net(rimmed, weights_of(1), halo))

    def coronal_only():
        return no_part, reflect_of(coronal_net(rounded, weights_of(2)))

    part, held = lax.switch(agent_place, [data_start, axial_only, sagittal_only, coronal_only])
    own_sinogram = sinogram.reshape(rays_here * slices, LANES)

    for step in range(DATA_STEPS):
        residual = ray_exchange(part, own_sinogram, tile_count)
        if step < DATA_STEPS - 1:

            def advance(held, residual):
                moved = held - 0.8 * spread_back(residual)
                return project(moved), moved

            part, held = lax.cond(is_data, advance, lambda h, r: (no_part, h), held, residual)
        else:

            def settle(held, residual):
                moved = held - 0.8 * spread_back(residual)
                return 2.0 * moved - current

            reflect = lax.cond(is_data, settle, lambda h, r: h, held, residual)

    sent = reflect.astype(jnp.bfloat16).reshape(slices * local_rows, image_columns)
    others = agent_sum(sent).reshape(reflect.shape)
    new_states = 0.5 * current + 0.25 * others - 0.25 * reflect
    return new_states[None]


def solution(mesh):
    placed = (
        P("agent", None, "tile", None),
        P("tile", None, None),
        P("tile", None, None),
        P("tile"),
        P("tile"),
        P("tile"),
        P(),
        P(),
        P(),
    )
    return jax.shard_map(
        per_device,
        mesh=mesh,
        in_specs=placed,
        out_specs=P("agent", None, "tile", None),
        check_vma=False,
    )
```

profile of v0, /device:TPU:0, one launch (start us, length us, event | category | flops | bytes accessed | tf_op | source)
XLA Modules:
  0.0 111.4 jit_solution(9447131949885852237)
XLA Ops:
  0.0 1.1 bitcast_convert_fusion
  1.1 4.9 %collective-permute-start = (bf16[4,4,512]{2,1,0:T(4,128)(2,1)S(1)}, bf16[4,4,512]{2,1,0:T(4,128)(2,1)S(1)}, u32[]{:S(2)}, u32[]{:S(2)}) collective-permute-start(bf16[4,4,512]{2,1,0:T(4,128)(2,1)S(1)} %get-tuple-element.355), channel_id=1, source_target_pairs={{0,1},{1,2},{2,3},{3,4},{4,5},{5,6},{6,7},{8,9},{9,10},{10,11},{11... | collective-permute-start | bytes 49160 | tf_op jit(solution)/shard_map/ppermute | solution.py:25
  6.0 1.3 %collective-permute-start.1 = (bf16[4,4,512]{2,1,0:T(4,128)(2,1)S(1)}, bf16[4,4,512]{2,1,0:T(4,128)(2,1)S(1)}, u32[]{:S(2)}, u32[]{:S(2)}) collective-permute-start(bf16[4,4,512]{2,1,0:T(4,128)(2,1)S(1)} %get-tuple-element.356), channel_id=1, source_target_pairs={{1,0},{2,1},{3,2},{4,3},{5,4},{6,5},{7,6},{9,8},{10,9},{11,10},{12... | collective-permute-start | bytes 49160 | tf_op jit(solution)/shard_map/ppermute | solution.py:27
  7.4 4.2 %collective-permute-done.1 = bf16[4,4,512]{2,1,0:T(4,128)(2,1)S(1)} collective-permute-done((bf16[4,4,512]{2,1,0:T(4,128)(2,1)S(1)}, bf16[4,4,512]{2,1,0:T(4,128)(2,1)S(1)}, u32[]{:S(2)}, u32[]{:S(2)}) %collective-permute-start.1) | collective-permute-done | bytes 16416 | tf_op jit(solution)/shard_map/ppermute | solution.py:27
  11.7 11.7 %conditional.3 = (bf16[8,128,128]{2,1,0:T(8,128)(2,1)S(1)}, f32[4,64,512]{2,0,1:T(4,128)}, f32[4,64,512]{2,1,0:T(8,128)S(1)}) conditional(s32[]{:T(128)} %clamp.3, (s32[256]{0:T(256)}, s32[256]{0:T(256)}, s32[256]{0:T(256)}, f32[4,64,512]{2,1,0:T(8,128)}, bf16[256,128,128]{2,1,0:T(8,128)(2,1)}) %tuple.107, ...), branch_computations={%region_0.0_spmd, %region_1.2_spmd.clone, %region_2.3_spmd, %regio... | conditional | flops 14496871424 | bytes 25851226 | solution.py:522
  11.8 2.2 %fusion.98 = (bf16[4,64,512]{2,0,1:T(4,128)(2,1)S(1)}, f32[4,64,512]{2,0,1:T(4,128)}) fusion(f32[4,64,512]{2,1,0:T(8,128)} %get-tuple-element.359), kind=kLoop, calls=%fused_computation.183 | loop fusion | flops 131072 | bytes 1310720 | tf_op jit(solution)/shard_map/cond/branch_0_fun/convert_element_type | solution.py:472
  14.6 7.8 %fusion.1 = f32[256,4,128]{2,1,0:T(4,128)S(1)} fusion(bf16[256,128,128]{2,1,0:T(8,128)(2,1)} %get-tuple-element.122, bf16[256,4,128]{2,0,1:T(8,128)(2,1)S(1)} %convolution_convert_fusion.1), kind=kOutput, calls=%fused_computation.3 | convolution fusion | flops 33554432 | bytes 9175040 | tf_op jit(solution)/shard_map/cond/branch_0_fun/bzp,bqp->bzq/dot_general | solution.py:476
  23.4 15.9 %ray_exchange.2 = bf16[8,128,128]{2,1,0:T(8,128)(2,1)S(1)} custom-call(bf16[8,128,128]{2,1,0:T(8,128)(2,1)S(1)} %get-tuple-element.177.part_ref, f32[128,128]{1,0:T(8,128)} %bitcast.437), custom_call_target="tpu_custom_call" | custom-call | tf_op jit(solution)/shard_map/ray_exchange/pallas_call | solution.py:372
  39.3 17.9 %conditional.4 = (bf16[8,128,128]{2,1,0:T(8,128)(2,1)S(1)}, f32[4,64,512]{2,1,0:T(8,128)S(1)}) conditional(s32[]{:T(128)} %convert_element_type.242, f32[4,64,512]{2,1,0:T(8,128)S(1)} %get-tuple-element.323, (s32[256]{0:T(256)}, s32[256]{0:T(256)}, s32[256]{0:T(256)}, bf16[8,128,128]{2,1,0:T(8,128)(2,1)S(1)}, bf16[256,128,128]{2,1,0:T(8,128)(2,1)}, ...), branch_computations={%region_4.5_spmd, %region_5.6_spmd} | conditional | flops 1007682048 | bytes 26225708 | solution.py:533
  39.3 0.8 multiply_add_fusion.1
  40.4 5.7 %fusion.36 = f32[256,4,128]{2,1,0:T(4,128)S(1)} fusion(bf16[256,128,128]{2,1,0:T(8,128)(2,1)} %get-tuple-element.164, bf16[256,4,128]{2,0,1:T(8,128)(2,1)S(1)} %convolution_convert_fusion.12), kind=kOutput, calls=%fused_computation.85 | convolution fusion | flops 33554432 | bytes 9175040 | tf_op jit(solution)/shard_map/cond/branch_1_fun/bzq,bqp->bzp/dot_general | solution.py:490
  46.1 0.7 fusion.31
  47.0 1.2 %fusion.99 = (bf16[4,64,512]{2,1,0:T(8,128)(2,1)S(1)}, f32[4,64,512]{2,1,0:T(8,128)S(1)}) fusion(f32[4,64,512]{2,1,0:T(8,128)S(1)} %mul.64, f32[4,64,512]{2,0,1:T(4,128)} %get-tuple-element.322), kind=kLoop, calls=%fused_computation.184 | loop fusion | flops 262144 | bytes 1835008 | tf_op jit(solution)/shard_map/cond/branch_1_fun/convert_element_type | solution.py:472
  48.7 7.8 %fusion.34 = f32[256,4,128]{2,1,0:T(4,128)S(1)} fusion(bf16[256,128,128]{2,1,0:T(8,128)(2,1)} %get-tuple-element.164, bf16[256,4,128]{2,0,1:T(8,128)(2,1)S(1)} %convolution_convert_fusion.11), kind=kOutput, calls=%fused_computation.83 | convolution fusion | flops 33554432 | bytes 9175040 | tf_op jit(solution)/shard_map/cond/branch_1_fun/bzp,bqp->bzq/dot_general | solution.py:476
  56.5 0.5 convolution_convert_fusion.10
  57.2 14.2 %ray_exchange.3 = bf16[8,128,128]{2,1,0:T(8,128)(2,1)S(1)} custom-call(bf16[8,128,128]{2,1,0:T(8,128)(2,1)S(1)} %get-tuple-element.179.part_ref, f32[128,128]{1,0:T(8,128)} %bitcast.438), custom_call_target="tpu_custom_call" | custom-call | tf_op jit(solution)/shard_map/ray_exchange/pallas_call | solution.py:372
  71.5 8.0 %conditional.5 = (f32[4,64,512]{2,1,0:T(8,128)S(1)}) conditional(s32[]{:T(128)} %convert_element_type.242, f32[4,64,512]{2,1,0:T(8,128)S(1)} %get-tuple-element.178, (s32[256]{0:T(256)}, s32[256]{0:T(256)}, bf16[8,128,128]{2,1,0:T(8,128)(2,1)S(1)}, bf16[256,128,128]{2,1,0:T(8,128)(2,1)}, s32[256]{0:T(256)}, /*index=5*/f32[4,64,512]{2,1,0:T(8,128)S(1)}, ...), branch_computations={%region_6.7_spmd, %region_7.8_spmd} | conditional | flops 504103424 | bytes 14951460 | solution.py:540
  71.5 0.7 multiply_add_fusion.2
  72.5 5.7 %fusion.51 = f32[256,4,128]{2,1,0:T(4,128)S(1)} fusion(bf16[256,128,128]{2,1,0:T(8,128)(2,1)} %get-tuple-element.169, bf16[256,4,128]{2,0,1:T(8,128)(2,1)S(1)} %convolution_convert_fusion.13), kind=kOutput, calls=%fused_computation.102 | convolution fusion | flops 33554432 | bytes 9175040 | tf_op jit(solution)/shard_map/cond/branch_1_fun/bzq,bqp->bzp/dot_general | solution.py:490
  78.1 0.7 fusion.49
  79.5 0.7 convert_element_type.244
  80.2 29.1 %agent_sum.1 = f32[256,512]{1,0:T(8,128)} custom-call(bf16[256,512]{1,0:T(8,128)(2,1)} %bitcast.425), custom_call_target="tpu_custom_call" | custom-call | tf_op jit(solution)/shard_map/agent_sum/pallas_call | solution.py:426
  109.4 1.1 broadcast_multiply_fusion
  110.4 1.0 subtract_bitcast_fusion
  (34 shorter events, 3.6 us)
Async XLA Ops:
  1.1 6.3 %collective-permute-start = (bf16[4,4,512]{2,1,0:T(4,128)(2,1)S(1)}, bf16[4,4,512]{2,1,0:T(4,128)(2,1)S(1)}, u32[]{:S(2)}, u32[]{:S(2)}) collective-permute-start(bf16[4,4,512]{2,1,0:T(4,128)(2,1)S(1)} %get-tuple-element.355), channel_id=1, source_target_pairs={{0,1},{1,2},{2,3},{3,4},{4,5},{5,6},{6,7},{8,9},{9,10},{10,11},{11... | collective-permute-start | bytes 49160 | tf_op jit(solution)/shard_map/ppermute | solution.py:25
  6.0 5.6 %collective-permute-start.1 = (bf16[4,4,512]{2,1,0:T(4,128)(2,1)S(1)}, bf16[4,4,512]{2,1,0:T(4,128)(2,1)S(1)}, u32[]{:S(2)}, u32[]{:S(2)}) collective-permute-start(bf16[4,4,512]{2,1,0:T(4,128)(2,1)S(1)} %get-tuple-element.356), channel_id=1, source_target_pairs={{1,0},{2,1},{3,2},{4,3},{5,4},{6,5},{7,6},{9,8},{10,9},{11,10},{12... | collective-permute-start | bytes 49160 | tf_op jit(solution)/shard_map/ppermute | solution.py:27
  11.8 2.5 %copy-start.16 = (s32[256]{0:T(256)S(1)}, s32[256]{0:T(256)}, u32[]{:S(2)}) copy-start(s32[256]{0:T(256)} %get-tuple-element.120) | copy-start | bytes 3076 | tf_op jit(solution)/shard_map/cond
  14.5 7.9 %copy-start.22 = (s32[256]{0:T(256)S(1)}, s32[256]{0:T(256)}, u32[]{:S(2)}) copy-start(s32[256]{0:T(256)} %get-tuple-element.118) | copy-start | bytes 3076 | tf_op jit(solution)/shard_map/cond
  14.5 7.9 %copy-start.23 = (s32[256]{0:T(256)S(1)}, s32[256]{0:T(256)}, u32[]{:S(2)}) copy-start(s32[256]{0:T(256)} %get-tuple-element.119) | copy-start | bytes 3076 | tf_op jit(solution)/shard_map/cond
  14.5 8.6 %copy-start.1 = (f32[4,64,512]{2,1,0:T(8,128)S(1)}, f32[4,64,512]{2,1,0:T(8,128)}, u32[]{:S(2)}) copy-start(f32[4,64,512]{2,1,0:T(8,128)} %get-tuple-element.359) | copy-start | bytes 1572868 | tf_op jit(solution)/shard_map/cond
  39.3 32.1 %copy-start = (f32[1,4,64,512]{3,2,1,0:T(8,128)S(1)}, f32[1,4,64,512]{3,2,1,0:T(8,128)}, u32[]{:S(2)}) copy-start(f32[1,4,64,512]{3,2,1,0:T(8,128)} %param.38) | copy-start | bytes 1572868
  40.4 5.7 %copy-start.17 = (s32[256]{0:T(256)S(1)}, s32[256]{0:T(256)}, u32[]{:S(2)}) copy-start(s32[256]{0:T(256)} %get-tuple-element.161) | copy-start | bytes 3076 | tf_op jit(solution)/shard_map/cond
  72.5 5.7 %copy-start.18 = (s32[256]{0:T(256)S(1)}, s32[256]{0:T(256)}, u32[]{:S(2)}) copy-start(s32[256]{0:T(256)} %get-tuple-element.170) | copy-start | bytes 3076 | tf_op jit(solution)/shard_map/cond
where the time goes:
time: 112 us; the launch traced here: 111 us
  Pallas kernels  59.2 us (53%)
  matrix products  30.3 us (27%)
  other arithmetic  9.3 us (8%)
  starting transfers between devices  6.19 us (6%)
  waiting for transfers between devices  4.32 us (4%)
  local copies, waits for them, and re-layouts  1.43 us (1%)
    pallas_call x2, Pallas kernels, ray_exchange(): pl.pallas_call(functools.partial(ray_kernel, count), out_shape=jax.ShapeD...  30.1 us
    pallas_call x1, Pallas kernels, agent_sum(): pl.pallas_call(agent_kernel, out_shape=jax.ShapeDtypeStruct(own.shape, jn...  29.1 us
    dot_general x2, matrix products, project(): jnp.einsum('bzp,bqp->bzq', picked, blocks, preferred_element_type=jnp.flo...  15.6 us
    dot_general x2, matrix products, spread_back(): jnp.einsum('bzq,bqp->bzp', picked, blocks, preferred_element_type=jnp.flo...  11.3 us
    ppermute x1, starting transfers between devices, extended(): lax.ppermute(tail, axis, [(i, (i + 1) % count) for i in range(ends)])  4.9 us
    ppermute x1, waiting for transfers between devices, extended(): lax.ppermute(head, axis, [((i + 1) % count, i) for i in range(ends)])  4.21 us
    convert_element_type x2, other arithmetic, project(): pixels = volume.astype(jnp.bfloat16).reshape(slices, tiles_here, LANES)  3.49 us
  transfers between devices with their start and end apart: 2, of which 2 were waited for; matrix products, arithmetic and copies ran while one was open for 0% of the time, Pallas kernels for 0%

commit v1 on v0

--- a/solution.py
+++ b/solution.py
@@ -226,7 +226,7 @@
         store(0, row, 1, y)
         return carry
 
-    lax.fori_loop(0, rows, first_step, 0)
+    lax.fori_loop(0, rows, first_step, 0, unroll=4)
     for layer in range(layers):
         source, target = layer % 2, (layer + 1) % 2
 

time: 112 us -> 102 us (0.911)
  Pallas kernels: 59.2 us -> 49.5 us
    pallas_call x1, Pallas kernels: 29.1 us -> 19.4 us  [agent_sum(): pl.pallas_call(agent_kernel, out_shape=jax.ShapeDtypeStruct(own.shape, jn...]
where the time goes in v1:
time: 102 us
  Pallas kernels  49.5 us (49%)
  matrix products  30.3 us (30%)
  other arithmetic  9.3 us (9%)
  starting transfers between devices  6.19 us (6%)
  waiting for transfers between devices  4.32 us (4%)
  local copies, waits for them, and re-layouts  1.43 us (1%)
    pallas_call x2, Pallas kernels, ray_exchange(): pl.pallas_call(functools.partial(ray_kernel, count), out_shape=jax.ShapeD...  30.1 us
    pallas_call x1, Pallas kernels, agent_sum(): pl.pallas_call(agent_kernel, out_shape=jax.ShapeDtypeStruct(own.shape, jn...  19.4 us
    dot_general x2, matrix products, project(): jnp.einsum('bzp,bqp->bzq', picked, blocks, preferred_element_type=jnp.flo...  15.6 us
    dot_general x2, matrix products, spread_back(): jnp.einsum('bzq,bqp->bzp', picked, blocks, preferred_element_type=jnp.flo...  11.3 us
    ppermute x1, starting transfers between devices, extended(): lax.ppermute(tail, axis, [(i, (i + 1) % count) for i in range(ends)])  4.9 us
    ppermute x1, waiting for transfers between devices, extended(): lax.ppermute(head, axis, [((i + 1) % count, i) for i in range(ends)])  4.21 us
    convert_element_type x2, other arithmetic, project(): pixels = volume.astype(jnp.bfloat16).reshape(slices, tiles_here, LANES)  3.49 us
  transfers between devices with their start and end apart: 2, of which 2 were waited for; matrix products, arithmetic and copies ran while one was open for 0% of the time, Pallas kernels for 0%

profile of v1, /device:TPU:0, one launch (start us, length us, event | category | flops | bytes accessed | tf_op | source)
XLA Modules:
  0.0 101.7 jit_solution(17438033776436263919)
XLA Ops:
  0.0 1.1 %bitcast_convert_fusion = bf16[4,64,512]{2,1,0:T(8,128)(2,1)S(1)} fusion(f32[1,4,64,512]{3,2,1,0:T(8,128)} %param.38), kind=kLoop, calls=%fused_computation.182 | loop fusion | flops 131072 | bytes 786432 | tf_op jit(solution)/shard_map/convert_element_type | solution.py:500
  1.1 4.9 %collective-permute-start = (bf16[4,4,512]{2,1,0:T(4,128)(2,1)S(1)}, bf16[4,4,512]{2,1,0:T(4,128)(2,1)S(1)}, u32[]{:S(2)}, u32[]{:S(2)}) collective-permute-start(bf16[4,4,512]{2,1,0:T(4,128)(2,1)S(1)} %get-tuple-element.355), channel_id=1, source_target_pairs={{0,1},{1,2},{2,3},{3,4},{4,5},{5,6},{6,7},{8,9},{9,10},{10,11},{11... | collective-permute-start | bytes 49160 | tf_op jit(solution)/shard_map/ppermute | solution.py:25
  6.0 1.3 %collective-permute-start.1 = (bf16[4,4,512]{2,1,0:T(4,128)(2,1)S(1)}, bf16[4,4,512]{2,1,0:T(4,128)(2,1)S(1)}, u32[]{:S(2)}, u32[]{:S(2)}) collective-permute-start(bf16[4,4,512]{2,1,0:T(4,128)(2,1)S(1)} %get-tuple-element.356), channel_id=1, source_target_pairs={{1,0},{2,1},{3,2},{4,3},{5,4},{6,5},{7,6},{9,8},{10,9},{11,10},{12... | collective-permute-start | bytes 49160 | tf_op jit(solution)/shard_map/ppermute | solution.py:27
  7.4 4.2 %collective-permute-done.1 = bf16[4,4,512]{2,1,0:T(4,128)(2,1)S(1)} collective-permute-done((bf16[4,4,512]{2,1,0:T(4,128)(2,1)S(1)}, bf16[4,4,512]{2,1,0:T(4,128)(2,1)S(1)}, u32[]{:S(2)}, u32[]{:S(2)}) %collective-permute-start.1) | collective-permute-done | bytes 16416 | tf_op jit(solution)/shard_map/ppermute | solution.py:27
  11.7 11.7 %conditional.3 = (bf16[8,128,128]{2,1,0:T(8,128)(2,1)S(1)}, f32[4,64,512]{2,0,1:T(4,128)}, f32[4,64,512]{2,1,0:T(8,128)S(1)}) conditional(s32[]{:T(128)} %clamp.3, (s32[256]{0:T(256)}, s32[256]{0:T(256)}, s32[256]{0:T(256)}, f32[4,64,512]{2,1,0:T(8,128)}, bf16[256,128,128]{2,1,0:T(8,128)(2,1)}) %tuple.107, ...), branch_computations={%region_0.0_spmd, %region_1.2_spmd.clone, %region_2.3_spmd, %regio... | conditional | flops 14496871424 | bytes 25851226 | solution.py:522
  11.8 2.2 %fusion.98 = (bf16[4,64,512]{2,0,1:T(4,128)(2,1)S(1)}, f32[4,64,512]{2,0,1:T(4,128)}) fusion(f32[4,64,512]{2,1,0:T(8,128)} %get-tuple-element.359), kind=kLoop, calls=%fused_computation.183 | loop fusion | flops 131072 | bytes 1310720 | tf_op jit(solution)/shard_map/cond/branch_0_fun/convert_element_type | solution.py:472
  14.6 7.8 %fusion.1 = f32[256,4,128]{2,1,0:T(4,128)S(1)} fusion(bf16[256,128,128]{2,1,0:T(8,128)(2,1)} %get-tuple-element.122, bf16[256,4,128]{2,0,1:T(8,128)(2,1)S(1)} %convolution_convert_fusion.1), kind=kOutput, calls=%fused_computation.3 | convolution fusion | flops 33554432 | bytes 9175040 | tf_op jit(solution)/shard_map/cond/branch_0_fun/bzp,bqp->bzq/dot_general | solution.py:476
  23.4 15.9 %ray_exchange.2 = bf16[8,128,128]{2,1,0:T(8,128)(2,1)S(1)} custom-call(bf16[8,128,128]{2,1,0:T(8,128)(2,1)S(1)} %get-tuple-element.177.part_ref, f32[128,128]{1,0:T(8,128)} %bitcast.437), custom_call_target="tpu_custom_call" | custom-call | tf_op jit(solution)/shard_map/ray_exchange/pallas_call | solution.py:372
  39.3 17.9 %conditional.4 = (bf16[8,128,128]{2,1,0:T(8,128)(2,1)S(1)}, f32[4,64,512]{2,1,0:T(8,128)S(1)}) conditional(s32[]{:T(128)} %convert_element_type.242, f32[4,64,512]{2,1,0:T(8,128)S(1)} %get-tuple-element.323, (s32[256]{0:T(256)}, s32[256]{0:T(256)}, s32[256]{0:T(256)}, bf16[8,128,128]{2,1,0:T(8,128)(2,1)S(1)}, bf16[256,128,128]{2,1,0:T(8,128)(2,1)}, ...), branch_computations={%region_4.5_spmd, %region_5.6_spmd} | conditional | flops 1007682048 | bytes 26225708 | solution.py:533
  39.3 0.8 multiply_add_fusion.1
  40.4 5.7 %fusion.36 = f32[256,4,128]{2,1,0:T(4,128)S(1)} fusion(bf16[256,128,128]{2,1,0:T(8,128)(2,1)} %get-tuple-element.164, bf16[256,4,128]{2,0,1:T(8,128)(2,1)S(1)} %convolution_convert_fusion.12), kind=kOutput, calls=%fused_computation.85 | convolution fusion | flops 33554432 | bytes 9175040 | tf_op jit(solution)/shard_map/cond/branch_1_fun/bzq,bqp->bzp/dot_general | solution.py:490
  46.1 0.7 fusion.31
  47.0 1.2 %fusion.99 = (bf16[4,64,512]{2,1,0:T(8,128)(2,1)S(1)}, f32[4,64,512]{2,1,0:T(8,128)S(1)}) fusion(f32[4,64,512]{2,1,0:T(8,128)S(1)} %mul.64, f32[4,64,512]{2,0,1:T(4,128)} %get-tuple-element.322), kind=kLoop, calls=%fused_computation.184 | loop fusion | flops 262144 | bytes 1835008 | tf_op jit(solution)/shard_map/cond/branch_1_fun/convert_element_type | solution.py:472
  48.7 7.8 %fusion.34 = f32[256,4,128]{2,1,0:T(4,128)S(1)} fusion(bf16[256,128,128]{2,1,0:T(8,128)(2,1)} %get-tuple-element.164, bf16[256,4,128]{2,0,1:T(8,128)(2,1)S(1)} %convolution_convert_fusion.11), kind=kOutput, calls=%fused_computation.83 | convolution fusion | flops 33554432 | bytes 9175040 | tf_op jit(solution)/shard_map/cond/branch_1_fun/bzp,bqp->bzq/dot_general | solution.py:476
  56.5 0.5 convolution_convert_fusion.10
  57.2 14.2 %ray_exchange.3 = bf16[8,128,128]{2,1,0:T(8,128)(2,1)S(1)} custom-call(bf16[8,128,128]{2,1,0:T(8,128)(2,1)S(1)} %get-tuple-element.179.part_ref, f32[128,128]{1,0:T(8,128)} %bitcast.438), custom_call_target="tpu_custom_call" | custom-call | tf_op jit(solution)/shard_map/ray_exchange/pallas_call | solution.py:372
  71.5 8.0 %conditional.5 = (f32[4,64,512]{2,1,0:T(8,128)S(1)}) conditional(s32[]{:T(128)} %convert_element_type.242, f32[4,64,512]{2,1,0:T(8,128)S(1)} %get-tuple-element.178, (s32[256]{0:T(256)}, s32[256]{0:T(256)}, bf16[8,128,128]{2,1,0:T(8,128)(2,1)S(1)}, bf16[256,128,128]{2,1,0:T(8,128)(2,1)}, s32[256]{0:T(256)}, /*index=5*/f32[4,64,512]{2,1,0:T(8,128)S(1)}, ...), branch_computations={%region_6.7_spmd, %region_7.8_spmd} | conditional | flops 504103424 | bytes 14951460 | solution.py:540
  71.5 0.7 multiply_add_fusion.2
  72.5 5.7 %fusion.51 = f32[256,4,128]{2,1,0:T(4,128)S(1)} fusion(bf16[256,128,128]{2,1,0:T(8,128)(2,1)} %get-tuple-element.169, bf16[256,4,128]{2,0,1:T(8,128)(2,1)S(1)} %convolution_convert_fusion.13), kind=kOutput, calls=%fused_computation.102 | convolution fusion | flops 33554432 | bytes 9175040 | tf_op jit(solution)/shard_map/cond/branch_1_fun/bzq,bqp->bzp/dot_general | solution.py:490
  78.1 0.7 fusion.49
  79.5 0.7 convert_element_type.244
  80.2 19.4 %agent_sum.1 = f32[256,512]{1,0:T(8,128)} custom-call(bf16[256,512]{1,0:T(8,128)(2,1)} %bitcast.425), custom_call_target="tpu_custom_call" | custom-call | tf_op jit(solution)/shard_map/agent_sum/pallas_call | solution.py:426
  99.7 1.1 %broadcast_multiply_fusion = f32[256,512]{1,0:T(8,128)S(1)} fusion(f32[256,512]{1,0:T(8,128)} %agent_sum.1), kind=kLoop, calls=%fused_computation.181 | loop fusion | flops 131072 | bytes 1048576 | tf_op jit(solution)/shard_map/mul | solution.py:544
  100.7 1.0 subtract_bitcast_fusion
  (34 shorter events, 3.6 us)
Async XLA Ops:
  1.1 6.3 %collective-permute-start = (bf16[4,4,512]{2,1,0:T(4,128)(2,1)S(1)}, bf16[4,4,512]{2,1,0:T(4,128)(2,1)S(1)}, u32[]{:S(2)}, u32[]{:S(2)}) collective-permute-start(bf16[4,4,512]{2,1,0:T(4,128)(2,1)S(1)} %get-tuple-element.355), channel_id=1, source_target_pairs={{0,1},{1,2},{2,3},{3,4},{4,5},{5,6},{6,7},{8,9},{9,10},{10,11},{11... | collective-permute-start | bytes 49160 | tf_op jit(solution)/shard_map/ppermute | solution.py:25
  6.0 5.6 %collective-permute-start.1 = (bf16[4,4,512]{2,1,0:T(4,128)(2,1)S(1)}, bf16[4,4,512]{2,1,0:T(4,128)(2,1)S(1)}, u32[]{:S(2)}, u32[]{:S(2)}) collective-permute-start(bf16[4,4,512]{2,1,0:T(4,128)(2,1)S(1)} %get-tuple-element.356), channel_id=1, source_target_pairs={{1,0},{2,1},{3,2},{4,3},{5,4},{6,5},{7,6},{9,8},{10,9},{11,10},{12... | collective-permute-start | bytes 49160 | tf_op jit(solution)/shard_map/ppermute | solution.py:27
  11.8 2.5 %copy-start.16 = (s32[256]{0:T(256)S(1)}, s32[256]{0:T(256)}, u32[]{:S(2)}) copy-start(s32[256]{0:T(256)} %get-tuple-element.120) | copy-start | bytes 3076 | tf_op jit(solution)/shard_map/cond
  14.5 7.9 %copy-start.22 = (s32[256]{0:T(256)S(1)}, s32[256]{0:T(256)}, u32[]{:S(2)}) copy-start(s32[256]{0:T(256)} %get-tuple-element.118) | copy-start | bytes 3076 | tf_op jit(solution)/shard_map/cond
  14.5 7.9 %copy-start.23 = (s32[256]{0:T(256)S(1)}, s32[256]{0:T(256)}, u32[]{:S(2)}) copy-start(s32[256]{0:T(256)} %get-tuple-element.119) | copy-start | bytes 3076 | tf_op jit(solution)/shard_map/cond
  14.5 8.6 %copy-start.1 = (f32[4,64,512]{2,1,0:T(8,128)S(1)}, f32[4,64,512]{2,1,0:T(8,128)}, u32[]{:S(2)}) copy-start(f32[4,64,512]{2,1,0:T(8,128)} %get-tuple-element.359) | copy-start | bytes 1572868 | tf_op jit(solution)/shard_map/cond
  39.3 32.1 %copy-start = (f32[1,4,64,512]{3,2,1,0:T(8,128)S(1)}, f32[1,4,64,512]{3,2,1,0:T(8,128)}, u32[]{:S(2)}) copy-start(f32[1,4,64,512]{3,2,1,0:T(8,128)} %param.38) | copy-start | bytes 1572868
  40.4 5.7 %copy-start.17 = (s32[256]{0:T(256)S(1)}, s32[256]{0:T(256)}, u32[]{:S(2)}) copy-start(s32[256]{0:T(256)} %get-tuple-element.161) | copy-start | bytes 3076 | tf_op jit(solution)/shard_map/cond
  72.5 5.7 %copy-start.18 = (s32[256]{0:T(256)S(1)}, s32[256]{0:T(256)}, u32[]{:S(2)}) copy-start(s32[256]{0:T(256)} %get-tuple-element.170) | copy-start | bytes 3076 | tf_op jit(solution)/shard_map/cond
